TPU v7x, 32 devices: a whole 2x2x4 slice. The times are simulated.
32 devices in a mesh: groups: 2 (over y), chain: 4 (over z), samp: 4 (over x, core).
Axes of the slice: x: 2, y: 2, z: 4, core: 2. Of those that a mesh axis runs over, the one named last changes fastest.
Arguments:
- dosage: bfloat16 [16384, 4096], P('samp', ('groups', 'chain')), parts along dimension 1
- filter_mask: int32 [4096], P(('groups', 'chain')), parts along dimension 0, may hold values 0 or 1
- counts: int32 [8], P(('groups', 'chain')), parts along dimension 0, may hold values from 128 to 512, as said below
Outputs:
- ld_tiles: float32 [8, 512, 3, 512], P(('groups', 'chain'), 'samp'), parts along dimension 0
There are 2 independent parts, one for each index of `groups`. A program takes and returns all parts, laid end to end along the dimension named above; each array names one. Nothing has to cross between parts.
Inputs may be any that keep to these rules, and one draw needn't show every extreme that they name: `counts`: every block but the last holds 512 live variants; the last holds from 128 to 512.
All inputs are finite; a program needn't handle non-finite values. No bound on the sum of `filter_mask` on one device may be relied on, other than what follows from the above.
Results may differ from a plain program's by a relative error of at most 0.0013.
Values may be sent and summed in bfloat16 or wider, within the bound.
A program may use at most 64 MiB of HBM per device.

v0:
```python
import functools

import jax
import jax.numpy as jnp
from jax import lax
from jax.experimental import pallas as pl
from jax.experimental.pallas import tpu as pltpu
from jax.sharding import PartitionSpec as P

MESH = pl.DeviceIdType.MESH
PARTS = 4


def remote(src, dst, send_sem, recv_sem, where):
    return pltpu.make_async_remote_copy(
        src_ref=src, dst_ref=dst, send_sem=send_sem, recv_sem=recv_sem,
        device_id=where, device_id_type=MESH,
    )


def kernel(n, peers, samples, dosage, mask, counts, near,
           own, left, right, own_t, left_t, part0, part1, part2, pair0, pair1, pair2, far0, far1, far2,
           sums, stats, moments, left_moments, right_moments, total2, far,
           load_sem, send_z, recv_z, send_m, recv_m, send_s, recv_s,
           send_a, recv_a, send_b, recv_b, send_f, recv_f):
    m = lax.axis_index("chain")
    me = lax.axis_index("samp")
    mine, odd = me // 2, me % 2
    rows, width = own.shape
    cut = width // peers
    deep = rows // PARTS
    has_left, has_right = m > 0, m < n - 1
    up, down = {"chain": m + 1}, {"chain": m - 1}

    load = pltpu.make_async_copy(dosage, own, load_sem)
    load.start()

    barrier = pltpu.get_barrier_semaphore()
    for r in range(peers):
        @pl.when(me != r)
        def _():
            pl.semaphore_signal(barrier, inc=1, device_id={"samp": r}, device_id_type=MESH)

    @pl.when(has_left)
    def _():
        pl.semaphore_signal(barrier, inc=1, device_id=down, device_id_type=MESH)

    @pl.when(has_right)
    def _():
        pl.semaphore_signal(barrier, inc=1, device_id=up, device_id_type=MESH)

    pl.semaphore_wait(barrier, peers - 1 + has_left.astype(jnp.int32) + has_right.astype(jnp.int32))

    def block_of(c, k):
        return pl.ds(pl.multiple_of(k * deep, deep), deep), pl.ds(c * cut, cut)

    def z_copy(way, c, k):
        at = block_of(c, k)
        return remote(dosage.at[at], (left, right)[way].at[at], send_z.at[way, c, k],
                      recv_z.at[way, c, k], (up, down)[way])

    def m_copy(way):
        return remote(moments, (left_moments, right_moments)[way], send_m.at[way],
                      recv_m.at[way], (up, down)[way])

    def each_way(action):
        for way, present in ((0, has_right), (1, has_left)):
            @pl.when(present)
            def _():
                action(way)

    def start_z(c):
        def go(way):
            for k in range(PARTS):
                z_copy(way, c, k).start()
        each_way(go)

    start_z(0)

    @pl.when(jnp.logical_not(has_left))
    def _():
        left[...] = jnp.zeros_like(left)
        left_moments[...] = jnp.zeros_like(left_moments)

    @pl.when(jnp.logical_not(has_right))
    def _():
        right[...] = jnp.zeros_like(right)
        right_moments[...] = jnp.zeros_like(right_moments)

    part0[...] = jnp.zeros_like(part0)
    part1[...] = jnp.zeros_like(part1)
    part2[...] = jnp.zeros_like(part2)
    load.wait()

    step = 64

    def add_up(i, carry):
        s, q = carry
        v = own[pl.ds(pl.multiple_of(i * step, step), step), :].astype(jnp.float32)
        v = v.reshape(step // 8, 8, width)
        return s + jnp.sum(v, 0), q + jnp.sum(v * v, 0)

    zero = jnp.zeros((8, width), jnp.float32)
    s, q = lax.fori_loop(0, rows // step, add_up, (zero, zero))
    sums[0:1, :] = jnp.sum(s, 0, keepdims=True)
    sums[1:2, :] = jnp.sum(q, 0, keepdims=True)

    def s_copy(r):
        return remote(sums, stats.at[me], send_s.at[r], recv_s.at[me], {"samp": r})

    def s_from(j):
        return remote(sums, stats.at[j], send_s.at[j], recv_s.at[j], {"samp": j})

    def others(action):
        for r in range(peers):
            @pl.when(me != r)
            def _():
                action(r)

    others(lambda r: s_copy(r).start())
    stats[me] = sums[...]
    others(lambda r: s_from(r).wait_recv())
    both = stats[0]
    for j in range(1, peers):
        both = both + stats[j]
    mean = both[0:1] / samples
    var = both[1:2] / samples - mean * mean
    live = (lax.broadcasted_iota(jnp.int32, (1, width), 1) < counts[0]).astype(jnp.float32)
    keep = mask[...].astype(jnp.float32) * live
    moments[0:1, :] = mean
    moments[1:2, :] = lax.rsqrt(var + 1e-05) * keep
    each_way(lambda way: m_copy(way).start())
    for c in range(1, peers):
        start_z(c)

    def standard(ref, at, which):
        v = ref[at].astype(jnp.float32)
        return (v - which[0:1, at[1]]) * which[1:2, at[1]]

    parts, pairs, fars = (part0, part1, part2), (pair0, pair1, pair2), (far0, far1, far2)

    def pair_copy(kind, c, r):
        columns = columns_of(kind, c, r)
        return remote(
            parts[kind].at[pl.ds(r * cut, cut), columns], pairs[kind].at[r // 2, :, columns],
            send_a.at[kind, c, r // 2], recv_a.at[kind, c, r // 2], {"samp": me + 1 - 2 * odd})

    def far_copy(kind, c, r, source):
        columns = columns_of(kind, c, r)
        return remote(
            pairs[kind].at[r // 2, :, columns], fars[kind].at[source, :, columns],
            send_b.at[kind, c, r // 2], recv_b.at[kind, c, source], {"samp": r})

    def columns_of(kind, c, r):
        if kind == 0:
            return pl.ds(0, width)
        if kind == 1 or r < c:
            return pl.ds(c * cut, cut)
        return pl.ds(0, (c + 1) * cut)

    def takes(kind, c):
        return range(c + 1) if kind == 2 else range(peers)

    def send_pairs(kind, c, wait=False):
        for r in takes(kind, c):
            @pl.when(odd != r % 2)
            def _():
                copy = pair_copy(kind, c, r)
                copy.wait_send() if wait else copy.start()

    def sum_pairs(kind, c):
        for r in takes(kind, c):
            @pl.when(odd == r % 2)
            def _():
                columns = columns_of(kind, c, r)
                pair_copy(kind, c, r).wait_recv()
                pairs[kind][r // 2, :, columns] += parts[kind][pl.ds(r * cut, cut), columns]

                @pl.when(mine != r // 2)
                def _():
                    far_copy(kind, c, r, mine).start()

    def sent_pairs(kind, c):
        for r in takes(kind, c):
            @pl.when(jnp.logical_and(odd == r % 2, mine != r // 2))
            def _():
                far_copy(kind, c, r, mine).wait_send()

    def ship(columns, c):
        return remote(total2.at[:, columns], far.at[:, columns], send_f.at[c], recv_f.at[c], down)

    def collect(kind, c):
        for r in takes(kind, c):
            @pl.when(me == r)
            def _():
                columns = columns_of(kind, c, r)
                whole = pairs[kind][r // 2, :, columns]
                for q in range(peers // 2):
                    if q != r // 2:
                        far_copy(kind, c, r, q).wait_recv()
                        whole = whole + fars[kind][q, :, columns]
                if kind < 2:
                    near[kind, :, columns] = whole
                else:
                    total2[:, columns] = whole

    def start_ship(c):
        for r in takes(2, c):
            @pl.when(jnp.logical_and(me == r, has_left))
            def _():
                ship(columns_of(2, c, r), c).start()

    def own_step(k, _):
        at = pl.ds(pl.multiple_of(k * deep, deep), deep)
        for c in range(peers):
            here = (at, pl.ds(c * cut, cut))
            z = standard(own, here, moments)
            own[here] = z.astype(jnp.bfloat16)
            own_t[pl.ds(c * cut, cut), at] = z.T.astype(jnp.bfloat16)
        part0[...] += jnp.dot(own_t[:, at], own[at, :], preferred_element_type=jnp.float32)
        return 0

    lax.fori_loop(0, PARTS, own_step, 0)
    send_pairs(0, 0)

    def wait_moments(way):
        m_copy(1 - way).wait_recv()

    each_way(wait_moments)

    for c in range(peers):
        def one(k, _, c=c):
            at, columns = here = block_of(c, k)
            earlier = ((2, c - 1), (1, c - 1)) if c else ((0, 0),)

            @pl.when(k == 1)
            def _():
                for which in earlier:
                    sum_pairs(*which)

            @pl.when(k == PARTS - 1)
            def _():
                for which in earlier:
                    collect(*which)

            @pl.when(has_left)
            def _():
                z_copy(0, c, k).wait_recv()

            left_t[columns, at] = standard(left, here, left_moments).T.astype(jnp.bfloat16)

            @pl.when(has_right)
            def _():
                z_copy(1, c, k).wait_recv()

            right[here] = standard(right, here, right_moments).astype(jnp.bfloat16)
            part1[:, columns] += jnp.dot(own_t[:, at], right[here], preferred_element_type=jnp.float32)
            top = pl.ds(0, (c + 1) * cut)
            part2[top, columns] += jnp.dot(left_t[top, at], right[here], preferred_element_type=jnp.float32)
            if c:
                front = pl.ds(0, c * cut)
                part2[columns, front] += jnp.dot(left_t[columns, at], right[at, front], preferred_element_type=jnp.float32)
            return 0

        lax.fori_loop(0, PARTS, one, 0)
        send_pairs(2, c)
        send_pairs(1, c)
    for c in range(peers - 1):
        start_ship(c)
    sum_pairs(2, peers - 1)
    sum_pairs(1, peers - 1)
    collect(2, peers - 1)
    start_ship(peers - 1)
    collect(1, peers - 1)

    for c in range(peers):
        for r in takes(2, c):
            @pl.when(jnp.logical_and(me == r, has_right))
            def _():
                ship(columns_of(2, c, r), c).wait_recv()

    near[2] = far[...]

    @pl.when(jnp.logical_not(has_right))
    def _():
        near[2] = jnp.zeros_like(far)

    others(lambda r: s_copy(r).wait_send())
    each_way(lambda way: m_copy(way).wait_send())
    for c in range(peers):
        def sent(way):
            for k in range(PARTS):
                z_copy(way, c, k).wait_send()
        each_way(sent)
        for kind in (1, 2):
            send_pairs(kind, c, True)
            sent_pairs(kind, c)
        for r in takes(2, c):
            @pl.when(jnp.logical_and(me == r, has_left))
            def _():
                ship(columns_of(2, c, r), c).wait_send()
    send_pairs(0, 0, True)
    sent_pairs(0, 0)


def body(n, peers, dosage, filter_mask, counts):
    rows, width = dosage.shape
    cut = width // peers
    samples = rows * peers
    f32, bf16 = jnp.float32, jnp.bfloat16
    vmem = pl.BlockSpec(memory_space=pltpu.VMEM)
    dma = pltpu.SemaphoreType.DMA
    tiles = pl.pallas_call(
        functools.partial(kernel, n, peers, samples),
        out_shape=jax.ShapeDtypeStruct((3, cut, width), f32),
        in_specs=[pl.BlockSpec(memory_space=pl.ANY), vmem, pl.BlockSpec(memory_space=pltpu.SMEM)],
        out_specs=vmem,
        scratch_shapes=[
            *[pltpu.VMEM((rows, width), bf16)] * 3,
            *[pltpu.VMEM((width, rows), bf16)] * 2,
            *[pltpu.VMEM((width, width), f32)] * 3,
            *[pltpu.VMEM((peers // 2, cut, width), f32)] * 6,
            pltpu.VMEM((2, width), f32),
            pltpu.VMEM((peers, 2, width), f32),
            *[pltpu.VMEM((2, width), f32)] * 3,
            *[pltpu.VMEM((cut, width), f32)] * 2,
            dma,
            *[dma((2, peers, PARTS))] * 2,
            *[dma((2,))] * 2,
            *[dma((peers,))] * 2,
            *[dma((3, peers, peers // 2))] * 4,
            *[dma((peers,))] * 2,
        ],
        compiler_params=pltpu.CompilerParams(
            collective_id=0, has_side_effects=True, vmem_limit_bytes=60 * 2**20),
    )(dosage, filter_mask[None], counts)
    return jnp.transpose(tiles / samples, (1, 0, 2))[None]


def solution(mesh):
    in_specs = (P("samp", ("groups", "chain")), P(("groups", "chain")), P(("groups", "chain")))
    out_specs = P(("groups", "chain"), "samp", None, None)
    run = functools.partial(body, mesh.shape["chain"], mesh.shape["samp"])
    return jax.shard_map(run, mesh=mesh, in_specs=in_specs, out_specs=out_specs, check_vma=False)
```

profile of v0, /device:TPU:3, one launch (start us, length us, event | category | flops | bytes accessed | tf_op | source)
XLA Modules:
  0.0 113.2 jit_solution(14705612821490947010)
XLA Ops:
  0.7 110.5 %shard_map.37 = f32[3,128,512]{2,1,0:T(8,128)} custom-call(bf16[4096,512]{1,0:T(8,128)(2,1)} %dosage.1, s32[1,512]{1,0:T(1,128)} %bitcast.5, s32[1]{0:T(128)S(6)} %copy.4.counts), custom_call_target="tpu_custom_call" | custom-call | tf_op jit(solution)/shard_map/pallas_call | solution.py:313
  111.1 2.1 %multiply_bitcast_fusion = f32[1,128,3,512]{3,1,2,0:T(8,128)} fusion(f32[3,128,512]{2,1,0:T(8,128)} %shard_map.37), kind=kLoop, calls=%fused_computation | loop fusion | flops 196608 | bytes 1572864 | tf_op jit(solution)/shard_map/broadcast_in_dim | solution.py:337
where the time goes:
time: 113 us
  Pallas kernels  110 us (97%)
  other arithmetic  2.09 us (2%)
    pallas_call x1, Pallas kernels, body(): pl.pallas_call(functools.partial(kernel, n, peers, samples), out_shape=ja...  110 us

commit v1 on v0

--- a/solution.py
+++ b/solution.py
@@ -9,6 +9,7 @@
 
 MESH = pl.DeviceIdType.MESH
 PARTS = 4
+FINE = 4
 
 
 def remote(src, dst, send_sem, recv_sem, where):
@@ -19,16 +20,22 @@
 
 
 def kernel(n, peers, samples, dosage, mask, counts, near,
-           own, left, right, own_t, left_t, part0, part1, part2, pair0, pair1, pair2, far0, far1, far2,
+           own, left, right, own_t, left_t, right_t,
+           part0, part1, part2, pair0, pair1, pair2, far0, far1, far2,
            sums, stats, moments, left_moments, right_moments, total2, far,
+           last1, last_rows, last_columns, out_rows, out_columns, land1, land_rows, land_columns,
            load_sem, send_z, recv_z, send_m, recv_m, send_s, recv_s,
-           send_a, recv_a, send_b, recv_b, send_f, recv_f):
+           send_a, recv_a, send_b, recv_b, send_f, recv_f,
+           send_1, recv_1, send_r, recv_r, send_c, recv_c):
     m = lax.axis_index("chain")
     me = lax.axis_index("samp")
     mine, odd = me // 2, me % 2
     rows, width = own.shape
     cut = width // peers
     deep = rows // PARTS
+    coarse = width - cut
+    fine = cut // FINE
+    middle = width - fine
     has_left, has_right = m > 0, m < n - 1
     up, down = {"chain": m + 1}, {"chain": m - 1}
 
@@ -58,6 +65,15 @@
         at = block_of(c, k)
         return remote(dosage.at[at], (left, right)[way].at[at], send_z.at[way, c, k],
                       recv_z.at[way, c, k], (up, down)[way])
+
+    slabs = ((coarse, cut - fine), (middle, fine))
+
+    def t_copy(way, f, k):
+        first, count = slabs[f]
+        at = pl.ds(pl.multiple_of(k * deep, deep), deep)
+        landing = (left_t.at[pl.ds(first, count), at], right_t.at[pl.ds(first - coarse, count), at])[way]
+        return remote(own_t.at[pl.ds(first, count), at], landing, send_z.at[way, peers - 1 + f, k],
+                      recv_z.at[way, peers - 1 + f, k], (up, down)[way])
 
     def m_copy(way):
         return remote(moments, (left_moments, right_moments)[way], send_m.at[way],
@@ -75,21 +91,32 @@
                 z_copy(way, c, k).start()
         each_way(go)
 
+    def start_t(f):
+        def go(way):
+            for k in range(PARTS):
+                t_copy(way, f, k).start()
+        each_way(go)
+
     start_z(0)
 
     @pl.when(jnp.logical_not(has_left))
     def _():
         left[...] = jnp.zeros_like(left)
+        left_t[coarse:, :] = jnp.zeros((cut, rows), left_t.dtype)
         left_moments[...] = jnp.zeros_like(left_moments)
 
     @pl.when(jnp.logical_not(has_right))
     def _():
         right[...] = jnp.zeros_like(right)
+        right_t[...] = jnp.zeros_like(right_t)
         right_moments[...] = jnp.zeros_like(right_moments)
 
     part0[...] = jnp.zeros_like(part0)
     part1[...] = jnp.zeros_like(part1)
     part2[...] = jnp.zeros_like(part2)
+    last1[...] = jnp.zeros_like(last1)
+    last_rows[...] = jnp.zeros_like(last_rows)
+    last_columns[...] = jnp.zeros_like(last_columns)
     load.wait()
 
     step = 64
@@ -130,7 +157,7 @@
     moments[0:1, :] = mean
     moments[1:2, :] = lax.rsqrt(var + 1e-05) * keep
     each_way(lambda way: m_copy(way).start())
-    for c in range(1, peers):
+    for c in range(1, peers - 1):
         start_z(c)
 
     def standard(ref, at, which):
@@ -202,7 +229,7 @@
                 if kind < 2:
                     near[kind, :, columns] = whole
                 else:
-                    total2[:, columns] = whole
+                    total2[:, columns] = whole.astype(total2.dtype)
 
     def start_ship(c):
         for r in takes(2, c):
@@ -228,7 +255,13 @@
 
     each_way(wait_moments)
 
-    for c in range(peers):
+    def across(a, b):
+        return lax.dot_general(a, b, (((1,), (1,)), ((), ())), preferred_element_type=jnp.float32)
+
+    def along(a, b):
+        return jnp.dot(a, b, preferred_element_type=jnp.float32)
+
+    for c in range(peers - 1):
         def one(k, _, c=c):
             at, columns = here = block_of(c, k)
             earlier = ((2, c - 1), (1, c - 1)) if c else ((0, 0),)
@@ -247,51 +280,166 @@
             def _():
                 z_copy(0, c, k).wait_recv()
 
-            left_t[columns, at] = standard(left, here, left_moments).T.astype(jnp.bfloat16)
+            z = standard(left, here, left_moments)
+            left[here] = z.astype(jnp.bfloat16)
+            left_t[columns, at] = z.T.astype(jnp.bfloat16)
 
             @pl.when(has_right)
             def _():
                 z_copy(1, c, k).wait_recv()
 
             right[here] = standard(right, here, right_moments).astype(jnp.bfloat16)
-            part1[:, columns] += jnp.dot(own_t[:, at], right[here], preferred_element_type=jnp.float32)
+            part1[:, columns] += along(own_t[:, at], right[here])
             top = pl.ds(0, (c + 1) * cut)
-            part2[top, columns] += jnp.dot(left_t[top, at], right[here], preferred_element_type=jnp.float32)
+            part2[top, columns] += along(left_t[top, at], right[here])
             if c:
                 front = pl.ds(0, c * cut)
-                part2[columns, front] += jnp.dot(left_t[columns, at], right[at, front], preferred_element_type=jnp.float32)
+                part2[columns, front] += along(left_t[columns, at], right[at, front])
             return 0
 
         lax.fori_loop(0, PARTS, one, 0)
         send_pairs(2, c)
         send_pairs(1, c)
-    for c in range(peers - 1):
-        start_ship(c)
+        if c == 0:
+            start_t(0)
+
+    def wait_slab(f, k):
+        @pl.when(has_left)
+        def _():
+            t_copy(0, f, k).wait_recv()
+
+        @pl.when(has_right)
+        def _():
+            t_copy(1, f, k).wait_recv()
+
+    whole_front, slab = pl.ds(0, coarse), pl.ds(coarse, cut - fine)
+
+    def first_slab(k, _):
+        at = pl.ds(pl.multiple_of(k * deep, deep), deep)
+
+        @pl.when(k == 1)
+        def _():
+            sum_pairs(2, peers - 2)
+            sum_pairs(1, peers - 2)
+
+        @pl.when(k == 2)
+        def _():
+            collect(2, peers - 2)
+            for c in range(peers - 1):
+                start_ship(c)
+            start_t(1)
+            collect(1, peers - 2)
+
+        wait_slab(0, k)
+        new = right_t[pl.ds(0, cut - fine), at]
+        part1[:, slab] += across(own_t[:, at], new)
+        part2[pl.ds(0, middle), slab] += across(left_t[pl.ds(0, middle), at], new)
+        part2[slab, whole_front] += along(left_t[slab, at], right[at, :])
+        return 0
+
+    lax.fori_loop(0, PARTS, first_slab, 0)
+    send_pairs(2, peers - 1)
+    send_pairs(1, peers - 1)
     sum_pairs(2, peers - 1)
     sum_pairs(1, peers - 1)
+
+    def last_slab(k, _):
+        at = pl.ds(pl.multiple_of(k * deep, deep), deep)
+        wait_slab(1, k)
+        new = right_t[pl.ds(cut - fine, fine), at]
+        last_columns[:, whole_front] += along(new, left[at, :])
+        last_columns[:, slab] += across(new, left_t[slab, at])
+        new_left = left_t[pl.ds(middle, fine), at]
+        last_rows[:, whole_front] += along(new_left, right[at, :])
+        last_rows[:, pl.ds(coarse, cut)] += across(new_left, right_t[:, at])
+        last1[...] += along(new, own[at, :])
+        return 0
+
+    lax.fori_loop(0, PARTS, last_slab, 0)
+
+    def columns_copy(r, source):
+        return remote(out_columns.at[:, pl.ds(r * cut, cut)], land_columns.at[source],
+                      send_c.at[r], recv_c.at[source], {"chain": m - 1, "samp": r})
+
+    def rows_copy(source):
+        return remote(out_rows, land_rows.at[source], send_r, recv_r.at[source],
+                      {"chain": m - 1, "samp": peers - 1})
+
+    def last1_copy(r, source):
+        return remote(last1.at[:, pl.ds(r * cut, cut)], land1.at[source],
+                      send_1.at[r], recv_1.at[source], {"samp": r})
+
+    out_columns[...] = last_columns[...].astype(out_columns.dtype)
+    out_rows[...] = last_rows[...].astype(out_rows.dtype)
+
+    @pl.when(has_left)
+    def _():
+        rows_copy(me).start()
+        for r in range(peers):
+            columns_copy(r, me).start()
+
+    others(lambda r: last1_copy(r, me).start())
+    for r in range(peers):
+        @pl.when(me == r)
+        def _():
+            land1[r] = last1[:, pl.ds(r * cut, cut)]
+
     collect(2, peers - 1)
     start_ship(peers - 1)
     collect(1, peers - 1)
 
-    for c in range(peers):
-        for r in takes(2, c):
-            @pl.when(jnp.logical_and(me == r, has_right))
-            def _():
-                ship(columns_of(2, c, r), c).wait_recv()
-
-    near[2] = far[...]
+    def turned(landed):
+        total = landed[0].astype(jnp.float32)
+        for j in range(1, peers):
+            total = total + landed[j].astype(jnp.float32)
+        return jnp.concatenate([jnp.zeros((cut - fine, cut), jnp.float32), total], 0).T
+
+    others(lambda r: last1_copy(r, r).wait_recv())
+    near[1, :, pl.ds(coarse, cut)] += turned(land1)
 
     @pl.when(jnp.logical_not(has_right))
     def _():
-        near[2] = jnp.zeros_like(far)
-
+        near[2] = jnp.zeros_like(near[2])
+
+    @pl.when(has_right)
+    def _():
+        for c in range(peers):
+            for r in takes(2, c):
+                @pl.when(me == r)
+                def _():
+                    ship(columns_of(2, c, r), c).wait_recv()
+        near[2] = far[...].astype(jnp.float32)
+        for source in range(peers):
+            columns_copy(0, source).wait_recv()
+        near[2, :, pl.ds(coarse, cut)] += turned(land_columns)
+
+        @pl.when(me == peers - 1)
+        def _():
+            total = jnp.zeros((fine, width), jnp.float32)
+            for source in range(peers):
+                rows_copy(source).wait_recv()
+                total = total + land_rows[source].astype(jnp.float32)
+            near[2, pl.ds(cut - fine, fine), :] += total
+
+    @pl.when(has_left)
+    def _():
+        rows_copy(me).wait_send()
+        for r in range(peers):
+            columns_copy(r, me).wait_send()
+
+    others(lambda r: last1_copy(r, me).wait_send())
     others(lambda r: s_copy(r).wait_send())
     each_way(lambda way: m_copy(way).wait_send())
+
+    def sent(way):
+        for k in range(PARTS):
+            for c in range(peers - 1):
+                z_copy(way, c, k).wait_send()
+            for f in range(2):
+                t_copy(way, f, k).wait_send()
+
+    each_way(sent)
     for c in range(peers):
-        def sent(way):
-            for k in range(PARTS):
-                z_copy(way, c, k).wait_send()
-        each_way(sent)
         for kind in (1, 2):
             send_pairs(kind, c, True)
             sent_pairs(kind, c)
@@ -306,6 +454,7 @@
 def body(n, peers, dosage, filter_mask, counts):
     rows, width = dosage.shape
     cut = width // peers
+    fine = cut // FINE
     samples = rows * peers
     f32, bf16 = jnp.float32, jnp.bfloat16
     vmem = pl.BlockSpec(memory_space=pltpu.VMEM)
@@ -316,23 +465,33 @@
         in_specs=[pl.BlockSpec(memory_space=pl.ANY), vmem, pl.BlockSpec(memory_space=pltpu.SMEM)],
         out_specs=vmem,
         scratch_shapes=[
-            *[pltpu.VMEM((rows, width), bf16)] * 3,
+            pltpu.VMEM((rows, width), bf16),
+            *[pltpu.VMEM((rows, width - cut), bf16)] * 2,
             *[pltpu.VMEM((width, rows), bf16)] * 2,
+            pltpu.VMEM((cut, rows), bf16),
             *[pltpu.VMEM((width, width), f32)] * 3,
             *[pltpu.VMEM((peers // 2, cut, width), f32)] * 6,
             pltpu.VMEM((2, width), f32),
             pltpu.VMEM((peers, 2, width), f32),
             *[pltpu.VMEM((2, width), f32)] * 3,
-            *[pltpu.VMEM((cut, width), f32)] * 2,
+            *[pltpu.VMEM((cut, width), bf16)] * 2,
+            *[pltpu.VMEM((fine, width), f32)] * 3,
+            *[pltpu.VMEM((fine, width), bf16)] * 2,
+            pltpu.VMEM((peers, fine, cut), f32),
+            pltpu.VMEM((peers, fine, width), bf16),
+            pltpu.VMEM((peers, fine, cut), bf16),
             dma,
-            *[dma((2, peers, PARTS))] * 2,
+            *[dma((2, peers + 1, PARTS))] * 2,
             *[dma((2,))] * 2,
             *[dma((peers,))] * 2,
             *[dma((3, peers, peers // 2))] * 4,
             *[dma((peers,))] * 2,
+            *[dma((peers,))] * 2,
+            dma, dma((peers,)),
+            *[dma((peers,))] * 2,
         ],
         compiler_params=pltpu.CompilerParams(
-            collective_id=0, has_side_effects=True, vmem_limit_bytes=60 * 2**20),
+            collective_id=0, has_side_effects=True, vmem_limit_bytes=52 * 2**20),
     )(dosage, filter_mask[None], counts)
     return jnp.transpose(tiles / samples, (1, 0, 2))[None]
 

time: 113 us -> 107 us (0.947); the launches traced: 113 us -> 106 us
  Pallas kernels: 110 us -> 103 us
  other arithmetic: 2.09 us -> 0.95 us
    pallas_call x1, Pallas kernels: 110 us -> 103 us  [body(): pl.pallas_call(functools.partial(kernel, n, peers, samples), out_shape=ja...]
    broadcast_in_dim x1, other arithmetic: 2.09 us -> 0.95 us  [body(): return jnp.transpose(tiles / samples, (1, 0, 2))[None]]
where the time goes in v1:
time: 107 us; the launch traced here: 106 us
  Pallas kernels  103 us (96%)
    pallas_call x1, Pallas kernels, body(): pl.pallas_call(functools.partial(kernel, n, peers, samples), out_shape=ja...  103 us

profile of v1, /device:TPU:3, one launch (start us, length us, event | category | flops | bytes accessed | tf_op | source)
XLA Modules:
  0.0 105.5 jit_solution(9567514792945972014)
XLA Ops:
  0.7 0.0 copy-start
  0.7 0.7 copy-done
  1.3 103.2 %shard_map.37 = f32[3,128,512]{2,1,0:T(8,128)S(1)} custom-call(bf16[4096,512]{1,0:T(8,128)(2,1)} %dosage.1, s32[1,512]{1,0:T(1,128)S(1)} %bitcast.5, s32[1]{0:T(128)S(6)} %copy.4.counts), custom_call_target="tpu_custom_call" | custom-call | tf_op jit(solution)/shard_map/pallas_call | solution.py:462
  104.6 0.9 multiply_bitcast_fusion
Async XLA Ops:
  0.7 0.7 copy-start

commit v2 on v1

--- a/solution.py
+++ b/solution.py
@@ -19,12 +19,12 @@
     )
 
 
-def kernel(n, peers, samples, dosage, mask, counts, near,
+def kernel(n, peers, samples, dosage, filter_mask, block_counts, near,
            own, left, right, own_t, left_t, right_t,
            part0, part1, part2, pair0, pair1, pair2, far0, far1, far2,
            sums, stats, moments, left_moments, right_moments, total2, far,
            last1, last_rows, last_columns, out_rows, out_columns, land1, land_rows, land_columns,
-           load_sem, send_z, recv_z, send_m, recv_m, send_s, recv_s,
+           mask, counts, mask_sem, counts_sem, load_sem, send_z, recv_z, send_m, recv_m, send_s, recv_s,
            send_a, recv_a, send_b, recv_b, send_f, recv_f,
            send_1, recv_1, send_r, recv_r, send_c, recv_c):
     m = lax.axis_index("chain")
@@ -41,6 +41,9 @@
 
     load = pltpu.make_async_copy(dosage, own, load_sem)
     load.start()
+    small = (pltpu.make_async_copy(filter_mask, mask, mask_sem), pltpu.make_async_copy(block_counts, counts, counts_sem))
+    for copy in small:
+        copy.start()
 
     barrier = pltpu.get_barrier_semaphore()
     for r in range(peers):
@@ -146,6 +149,8 @@
 
     others(lambda r: s_copy(r).start())
     stats[me] = sums[...]
+    for copy in small:
+        copy.wait()
     others(lambda r: s_from(r).wait_recv())
     both = stats[0]
     for j in range(1, peers):
@@ -302,6 +307,7 @@
         send_pairs(1, c)
         if c == 0:
             start_t(0)
+            start_t(1)
 
     def wait_slab(f, k):
         @pl.when(has_left)
@@ -327,7 +333,6 @@
             collect(2, peers - 2)
             for c in range(peers - 1):
                 start_ship(c)
-            start_t(1)
             collect(1, peers - 2)
 
         wait_slab(0, k)
@@ -462,7 +467,7 @@
     tiles = pl.pallas_call(
         functools.partial(kernel, n, peers, samples),
         out_shape=jax.ShapeDtypeStruct((3, cut, width), f32),
-        in_specs=[pl.BlockSpec(memory_space=pl.ANY), vmem, pl.BlockSpec(memory_space=pltpu.SMEM)],
+        in_specs=[pl.BlockSpec(memory_space=pl.ANY)] * 3,
         out_specs=vmem,
         scratch_shapes=[
             pltpu.VMEM((rows, width), bf16),
@@ -480,7 +485,9 @@
             pltpu.VMEM((peers, fine, cut), f32),
             pltpu.VMEM((peers, fine, width), bf16),
             pltpu.VMEM((peers, fine, cut), bf16),
-            dma,
+            pltpu.VMEM((1, width), jnp.int32),
+            pltpu.SMEM((1,), jnp.int32),
+            *[dma] * 3,
             *[dma((2, peers + 1, PARTS))] * 2,
             *[dma((2,))] * 2,
             *[dma((peers,))] * 2,
@@ -492,7 +499,7 @@
         ],
         compiler_params=pltpu.CompilerParams(
             collective_id=0, has_side_effects=True, vmem_limit_bytes=52 * 2**20),
-    )(dosage, filter_mask[None], counts)
+    )(dosage, pltpu.with_memory_space_constraint(filter_mask[None], pltpu.HBM), counts)
     return jnp.transpose(tiles / samples, (1, 0, 2))[None]
 
 

time: 107 us -> 105 us (0.981)
  no operation moved by 1% of the time
where the time goes in v2:
time: 105 us; the launch traced here: 104 us
  Pallas kernels  103 us (98%)
    pallas_call x1, Pallas kernels, body(): pl.pallas_call(functools.partial(kernel, n, peers, samples), out_shape=ja...  103 us

profile of v2, /device:TPU:3, one launch (start us, length us, event | category | flops | bytes accessed | tf_op | source)
XLA Modules:
  0.0 104.4 jit_solution(6469341835757917051)
XLA Ops:
  0.7 102.8 %shard_map.37 = f32[3,128,512]{2,1,0:T(8,128)S(1)} custom-call(bf16[4096,512]{1,0:T(8,128)(2,1)} %dosage.1, s32[1,512]{1,0:T(1,128)} %bitcast.5, s32[1]{0:T(128)S(6)} %copy.4.block_counts), custom_call_target="tpu_custom_call" | custom-call | tf_op jit(solution)/shard_map/pallas_call | solution.py:467
  103.4 1.0 multiply_bitcast_fusion

commit v3 on v2

--- a/solution.py
+++ b/solution.py
@@ -9,6 +9,7 @@
 
 MESH = pl.DeviceIdType.MESH
 PARTS = 4
+LAST_PARTS = 2
 FINE = 4
 
 
@@ -39,26 +40,26 @@
     has_left, has_right = m > 0, m < n - 1
     up, down = {"chain": m + 1}, {"chain": m - 1}
 
+    barrier = pltpu.get_barrier_semaphore()
+    for r in range(peers):
+        @pl.when(me != r)
+        def _():
+            pl.semaphore_signal(barrier, inc=1, device_id={"samp": r}, device_id_type=MESH)
+
+    @pl.when(has_left)
+    def _():
+        pl.semaphore_signal(barrier, inc=1, device_id=down, device_id_type=MESH)
+
+    @pl.when(has_right)
+    def _():
+        pl.semaphore_signal(barrier, inc=1, device_id=up, device_id_type=MESH)
+
     load = pltpu.make_async_copy(dosage, own, load_sem)
     load.start()
     small = (pltpu.make_async_copy(filter_mask, mask, mask_sem), pltpu.make_async_copy(block_counts, counts, counts_sem))
     for copy in small:
         copy.start()
 
-    barrier = pltpu.get_barrier_semaphore()
-    for r in range(peers):
-        @pl.when(me != r)
-        def _():
-            pl.semaphore_signal(barrier, inc=1, device_id={"samp": r}, device_id_type=MESH)
-
-    @pl.when(has_left)
-    def _():
-        pl.semaphore_signal(barrier, inc=1, device_id=down, device_id_type=MESH)
-
-    @pl.when(has_right)
-    def _():
-        pl.semaphore_signal(barrier, inc=1, device_id=up, device_id_type=MESH)
-
     pl.semaphore_wait(barrier, peers - 1 + has_left.astype(jnp.int32) + has_right.astype(jnp.int32))
 
     def block_of(c, k):
@@ -69,11 +70,15 @@
         return remote(dosage.at[at], (left, right)[way].at[at], send_z.at[way, c, k],
                       recv_z.at[way, c, k], (up, down)[way])
 
-    slabs = ((coarse, cut - fine), (middle, fine))
+    slabs = ((coarse, cut - fine, PARTS), (middle, fine, LAST_PARTS))
+
+    def piece(f, k):
+        size = rows // slabs[f][2]
+        return pl.ds(pl.multiple_of(k * size, size), size)
 
     def t_copy(way, f, k):
-        first, count = slabs[f]
-        at = pl.ds(pl.multiple_of(k * deep, deep), deep)
+        first, count, _ = slabs[f]
+        at = piece(f, k)
         landing = (left_t.at[pl.ds(first, count), at], right_t.at[pl.ds(first - coarse, count), at])[way]
         return remote(own_t.at[pl.ds(first, count), at], landing, send_z.at[way, peers - 1 + f, k],
                       recv_z.at[way, peers - 1 + f, k], (up, down)[way])
@@ -96,7 +101,7 @@
 
     def start_t(f):
         def go(way):
-            for k in range(PARTS):
+            for k in range(slabs[f][2]):
                 t_copy(way, f, k).start()
         each_way(go)
 
@@ -172,16 +177,19 @@
     parts, pairs, fars = (part0, part1, part2), (pair0, pair1, pair2), (far0, far1, far2)
 
     def pair_copy(kind, c, r):
-        columns = columns_of(kind, c, r)
+        columns, tall = columns_of(kind, c, r), height(kind, c, r)
         return remote(
-            parts[kind].at[pl.ds(r * cut, cut), columns], pairs[kind].at[r // 2, :, columns],
+            parts[kind].at[pl.ds(r * cut, tall), columns], pairs[kind].at[r // 2, pl.ds(0, tall), columns],
             send_a.at[kind, c, r // 2], recv_a.at[kind, c, r // 2], {"samp": me + 1 - 2 * odd})
 
     def far_copy(kind, c, r, source):
-        columns = columns_of(kind, c, r)
+        columns, tall = columns_of(kind, c, r), pl.ds(0, height(kind, c, r))
         return remote(
-            pairs[kind].at[r // 2, :, columns], fars[kind].at[source, :, columns],
+            pairs[kind].at[r // 2, tall, columns], fars[kind].at[source, tall, columns],
             send_b.at[kind, c, r // 2], recv_b.at[kind, c, source], {"samp": r})
+
+    def height(kind, c, r):
+        return cut - fine if (kind, c, r) == (2, peers - 1, peers - 1) else cut
 
     def columns_of(kind, c, r):
         if kind == 0:
@@ -204,9 +212,9 @@
         for r in takes(kind, c):
             @pl.when(odd == r % 2)
             def _():
-                columns = columns_of(kind, c, r)
+                columns, tall = columns_of(kind, c, r), height(kind, c, r)
                 pair_copy(kind, c, r).wait_recv()
-                pairs[kind][r // 2, :, columns] += parts[kind][pl.ds(r * cut, cut), columns]
+                pairs[kind][r // 2, :tall, columns] += parts[kind][pl.ds(r * cut, tall), columns]
 
                 @pl.when(mine != r // 2)
                 def _():
@@ -218,29 +226,30 @@
             def _():
                 far_copy(kind, c, r, mine).wait_send()
 
-    def ship(columns, c):
-        return remote(total2.at[:, columns], far.at[:, columns], send_f.at[c], recv_f.at[c], down)
+    def ship(c, r):
+        at = pl.ds(0, height(2, c, r)), columns_of(2, c, r)
+        return remote(total2.at[at], far.at[at], send_f.at[c], recv_f.at[c], down)
 
     def collect(kind, c):
         for r in takes(kind, c):
             @pl.when(me == r)
             def _():
-                columns = columns_of(kind, c, r)
-                whole = pairs[kind][r // 2, :, columns]
+                columns, tall = columns_of(kind, c, r), height(kind, c, r)
+                whole = pairs[kind][r // 2, :tall, columns]
                 for q in range(peers // 2):
                     if q != r // 2:
                         far_copy(kind, c, r, q).wait_recv()
-                        whole = whole + fars[kind][q, :, columns]
+                        whole = whole + fars[kind][q, :tall, columns]
                 if kind < 2:
                     near[kind, :, columns] = whole
                 else:
-                    total2[:, columns] = whole.astype(total2.dtype)
+                    total2[:tall, columns] = whole.astype(total2.dtype)
 
     def start_ship(c):
         for r in takes(2, c):
             @pl.when(jnp.logical_and(me == r, has_left))
             def _():
-                ship(columns_of(2, c, r), c).start()
+                ship(c, r).start()
 
     def own_step(k, _):
         at = pl.ds(pl.multiple_of(k * deep, deep), deep)
@@ -321,7 +330,7 @@
     whole_front, slab = pl.ds(0, coarse), pl.ds(coarse, cut - fine)
 
     def first_slab(k, _):
-        at = pl.ds(pl.multiple_of(k * deep, deep), deep)
+        at = piece(0, k)
 
         @pl.when(k == 1)
         def _():
@@ -346,10 +355,14 @@
     send_pairs(2, peers - 1)
     send_pairs(1, peers - 1)
     sum_pairs(2, peers - 1)
-    sum_pairs(1, peers - 1)
 
     def last_slab(k, _):
-        at = pl.ds(pl.multiple_of(k * deep, deep), deep)
+        at = piece(1, k)
+
+        @pl.when(k == LAST_PARTS - 1)
+        def _():
+            sum_pairs(1, peers - 1)
+
         wait_slab(1, k)
         new = right_t[pl.ds(cut - fine, fine), at]
         last_columns[:, whole_front] += along(new, left[at, :])
@@ -360,7 +373,7 @@
         last1[...] += along(new, own[at, :])
         return 0
 
-    lax.fori_loop(0, PARTS, last_slab, 0)
+    lax.fori_loop(0, LAST_PARTS, last_slab, 0)
 
     def columns_copy(r, source):
         return remote(out_columns.at[:, pl.ds(r * cut, cut)], land_columns.at[source],
@@ -412,11 +425,12 @@
             for r in takes(2, c):
                 @pl.when(me == r)
                 def _():
-                    ship(columns_of(2, c, r), c).wait_recv()
-        near[2] = far[...].astype(jnp.float32)
-        for source in range(peers):
-            columns_copy(0, source).wait_recv()
-        near[2, :, pl.ds(coarse, cut)] += turned(land_columns)
+                    ship(c, r).wait_recv()
+        near[2, :cut - fine] = far[:cut - fine].astype(jnp.float32)
+
+        @pl.when(me != peers - 1)
+        def _():
+            near[2, cut - fine:] = far[cut - fine:].astype(jnp.float32)
 
         @pl.when(me == peers - 1)
         def _():
@@ -424,7 +438,11 @@
             for source in range(peers):
                 rows_copy(source).wait_recv()
                 total = total + land_rows[source].astype(jnp.float32)
-            near[2, pl.ds(cut - fine, fine), :] += total
+            near[2, cut - fine:] = total
+
+        for source in range(peers):
+            columns_copy(0, source).wait_recv()
+        near[2, :, pl.ds(coarse, cut)] += turned(land_columns)
 
     @pl.when(has_left)
     def _():
@@ -440,7 +458,8 @@
         for k in range(PARTS):
             for c in range(peers - 1):
                 z_copy(way, c, k).wait_send()
-            for f in range(2):
+        for f in range(2):
+            for k in range(slabs[f][2]):
                 t_copy(way, f, k).wait_send()
 
     each_way(sent)
@@ -451,7 +470,7 @@
         for r in takes(2, c):
             @pl.when(jnp.logical_and(me == r, has_left))
             def _():
-                ship(columns_of(2, c, r), c).wait_send()
+                ship(c, r).wait_send()
     send_pairs(0, 0, True)
     sent_pairs(0, 0)
 
@@ -488,7 +507,7 @@
             pltpu.VMEM((1, width), jnp.int32),
             pltpu.SMEM((1,), jnp.int32),
             *[dma] * 3,
-            *[dma((2, peers + 1, PARTS))] * 2,
+            *[dma((2, peers + 1, max(PARTS, LAST_PARTS)))] * 2,
             *[dma((2,))] * 2,
             *[dma((peers,))] * 2,
             *[dma((3, peers, peers // 2))] * 4,
@@ -499,7 +518,7 @@
         ],
         compiler_params=pltpu.CompilerParams(
             collective_id=0, has_side_effects=True, vmem_limit_bytes=52 * 2**20),
-    )(dosage, pltpu.with_memory_space_constraint(filter_mask[None], pltpu.HBM), counts)
+    )(*[pltpu.with_memory_space_constraint(a, pltpu.HBM) for a in (dosage, filter_mask[None])], counts)
     return jnp.transpose(tiles / samples, (1, 0, 2))[None]
 
 

time: 105 us -> 106 us (level); the launches traced: 104 us -> 104 us
  no operation moved by 1% of the time
where the time goes in v3:
time: 106 us; the launch traced here: 104 us
  Pallas kernels  102 us (96%)
    pallas_call x1, Pallas kernels, body(): pl.pallas_call(functools.partial(kernel, n, peers, samples), out_shape=ja...  102 us

profile of v3, /device:TPU:3, one launch (start us, length us, event | category | flops | bytes accessed | tf_op | source)
XLA Modules:
  0.0 103.9 jit_solution(16060401834858643556)
XLA Ops:
  0.7 102.3 %shard_map.37 = f32[3,128,512]{2,1,0:T(8,128)S(1)} custom-call(bf16[4096,512]{1,0:T(8,128)(2,1)} %dosage.1, s32[1,512]{1,0:T(1,128)} %bitcast.5, s32[1]{0:T(128)S(6)} %copy.4.block_counts), custom_call_target="tpu_custom_call" | custom-call | tf_op jit(solution)/shard_map/pallas_call | solution.py:486
  102.9 1.0 multiply_bitcast_fusion
